TPU v7x, 32 devices: a whole 2x2x4 slice. The times are simulated.
32 devices in a mesh: gx: 2 (over y), gy: 4 (over z), gz: 4 (over x, core).
Axes of the slice: x: 2, y: 2, z: 4, core: 2. Of those that a mesh axis runs over, the one named last changes fastest.
Arguments:
- kappa_sq: float32 [32, 64, 512], P('gx', 'gz', 'gy'), may hold values from 0.004 to 0.4
- probe_bits: int32 [4, 32, 64, 512], P(None, 'gx', 'gz', 'gy'), may hold values from 0 to 1
Outputs:
- solution: float32 [4, 32, 64, 512], P(None, 'gx', 'gz', 'gy')
- relative_residual: float32 [4], replicated
All inputs are finite; a program needn't handle non-finite values.
Results may differ from a plain program's by a relative error of at most 0.0001.
Values sent between devices are 32-bit elements; how exact they have to be, the bound alone decides.
A program may use at most 128 MiB of HBM per device.

v0:
```python
import jax
import jax.numpy as jnp
from jax import lax
from jax.sharding import PartitionSpec as P

LEVELS = 3
COARSE_SWEEPS = 8
ITERS = 2


damping = 0.8


def extended(block, sides, width):
    for axis, dim in sides:
        count = lax.axis_size(axis)
        forward = [(i, i + 1) for i in range(count - 1)]
        backward = [(target, source) for source, target in forward]
        low = lax.ppermute(
            lax.slice_in_dim(block, block.shape[dim] - width, None, axis=dim), axis, forward
        )
        high = lax.ppermute(lax.slice_in_dim(block, 0, width, axis=dim), axis, backward)
        block = jnp.concatenate([low, block, high], axis=dim)
    return block


def neighbours(padded):
    along_first = padded[..., 2:, 1:-1, 1:-1] + padded[..., :-2, 1:-1, 1:-1]
    along_second = padded[..., 1:-1, 2:, 1:-1] + padded[..., 1:-1, :-2, 1:-1]
    along_third = padded[..., 1:-1, 1:-1, 2:] + padded[..., 1:-1, 1:-1, :-2]
    return along_first + along_second + along_third


def coarsen(field):
    leading = field.shape[:-3]
    cells_first, cells_second, cells_third = field.shape[-3:]
    grouped = field.reshape(
        leading + (cells_first // 2, 2, cells_second // 2, 2, cells_third // 2, 2)
    )
    return jnp.mean(grouped, axis=(-5, -3, -1))


def refine(field):
    leading = field.shape[:-3]
    cells_first, cells_second, cells_third = field.shape[-3:]
    spread = field.reshape(leading + (cells_first, 1, cells_second, 1, cells_third, 1))
    spread = jnp.broadcast_to(spread, leading + (cells_first, 2, cells_second, 2, cells_third, 2))
    return spread.reshape(leading + (cells_first * 2, cells_second * 2, cells_third * 2))


def level_faces(field, grid_level):
    if grid_level == 0:
        return extended(field, (("gx", 1), ("gy", 3), ("gz", 2)), 1)
    return extended(field, (("gx", 1), ("gy", 3), ("gz", 2)), 1)


def operate(field, diagonal, coupling, grid_level):
    return diagonal * field - coupling * neighbours(level_faces(field, grid_level))


def jacobi_sweep(field, rhs_field, diagonal, coupling, grid_level):
    return field + damping * (rhs_field - operate(field, diagonal, coupling, grid_level)) / diagonal


def assemble(gathered):
    count_x = lax.axis_size("gx")
    count_y = lax.axis_size("gy")
    count_z = lax.axis_size("gz")
    leading = gathered.shape[1:-3]
    cells_first, cells_second, cells_third = gathered.shape[-3:]
    lead_count = len(leading)
    blocks = gathered.reshape(
        (count_x, count_y, count_z) + leading + (cells_first, cells_second, cells_third)
    )
    permutation = tuple(range(3, 3 + lead_count)) + (
        0,
        3 + lead_count,
        2,
        4 + lead_count,
        1,
        5 + lead_count,
    )
    blocks = jnp.transpose(blocks, permutation)
    return blocks.reshape(
        leading + (count_x * cells_first, count_z * cells_second, count_y * cells_third)
    )


def local_dot(first_field, second_field):
    return jnp.sum(first_field * second_field, axis=(1, 2, 3))


def expand(values):
    return values[:, None, None, None]


def per_device(kappa_sq, probe_bits):
    diagonals = []
    couplings = []
    coef_field = kappa_sq
    for grid_level in range(LEVELS + 1):
        if grid_level > 0:
            coef_field = coarsen(coef_field)
        coupling = 0.25**grid_level
        diagonals.append(coef_field + 6.0 * coupling)
        couplings.append(coupling)
    global_diag = assemble(
        lax.all_gather(diagonals[LEVELS][None], ("gx", "gy", "gz"), axis=0, tiled=True)
    )

    def coarsest(rhs_field):
        diagonal = diagonals[LEVELS]
        coupling = couplings[LEVELS]
        global_rhs = assemble(
            lax.all_gather(rhs_field[None], ("gx", "gy", "gz"), axis=0, tiled=True)
        )
        field = damping * global_rhs / global_diag
        for sweep_index in range(COARSE_SWEEPS - 1):
            padded = jnp.pad(field, ((0, 0), (1, 1), (1, 1), (1, 1)))
            field = (
                field
                + damping
                * (global_rhs - (global_diag * field - coupling * neighbours(padded)))
                / global_diag
            )
        probes, block_x, block_z, block_y = rhs_field.shape
        zero_index = jnp.zeros((), jnp.int32)
        starts = (
            zero_index,
            lax.axis_index("gx") * block_x,
            lax.axis_index("gz") * block_z,
            lax.axis_index("gy") * block_y,
        )
        return lax.dynamic_slice(field, starts, (probes, block_x, block_z, block_y))

    def vcycle(rhs_field, grid_level):
        if grid_level == LEVELS:
            return coarsest(rhs_field)
        diagonal = diagonals[grid_level]
        coupling = couplings[grid_level]
        field = damping * rhs_field / diagonal
        field = jacobi_sweep(field, rhs_field, diagonal, coupling, grid_level)
        remainder = rhs_field - operate(field, diagonal, coupling, grid_level)
        field = field + refine(vcycle(coarsen(remainder), grid_level + 1))
        field = jacobi_sweep(field, rhs_field, diagonal, coupling, grid_level)
        return jacobi_sweep(field, rhs_field, diagonal, coupling, grid_level)

    right_side = 2.0 * probe_bits.astype(jnp.float32) - 1.0
    solution = jnp.zeros_like(right_side)
    residual = right_side
    fine_diag = diagonals[0]

    def precond_sum(first_field, second_field):
        return lax.psum(local_dot(first_field, second_field), ("gx", "gy", "gz"))

    precond = vcycle(residual, 0)
    precond_dot = precond_sum(residual, precond)
    search = precond
    for iteration in range(ITERS):
        operated = operate(search, fine_diag, 1.0, 0)
        step_size = precond_dot / lax.psum(local_dot(search, operated), ("gx", "gy", "gz"))
        solution = solution + expand(step_size) * search
        residual = residual - expand(step_size) * operated
        if iteration + 1 < ITERS:
            precond = vcycle(residual, 0)
            next_dot = precond_sum(residual, precond)
            search = precond + expand(next_dot / precond_dot) * search
            precond_dot = next_dot
    squares = lax.psum(local_dot(residual, residual), ("gx", "gy", "gz"))
    cell_total = (
        probe_bits.shape[1]
        * probe_bits.shape[2]
        * probe_bits.shape[3]
        * lax.axis_size("gx")
        * lax.axis_size("gy")
        * lax.axis_size("gz")
    )
    return (solution, jnp.sqrt(squares / cell_total))


def solution(mesh):
    return jax.shard_map(
        per_device,
        mesh=mesh,
        in_specs=(P("gx", "gz", "gy"), P(None, "gx", "gz", "gy")),
        out_specs=(P(None, "gx", "gz", "gy"), P()),
        check_vma=False,
    )
```

profile of v0, /device:TPU:0, one launch (start us, length us, event | category | flops | bytes accessed | tf_op | source)
XLA Modules:
  0.0 1080.7 jit_solution(16804115378510842129)
XLA Ops:
  2.7 4.9 collective-permute-start.1
  16.0 4.5 collective-permute-start.2
  40.4 4.8 collective-permute-start.8
  45.2 9.7 reshape.124
  69.1 8.8 copy.1882
  77.9 11.7 %reduce_sum.126 = f32[4,8,8,64]{0,3,2,1:T(8,128)S(1)} reduce(f32[4,8,2,8,2,64,2]{0,6,5,4,3,2,1:T(2,128)} %bitcast.21, f32[]{:T(128)} %constant.28.clone.1), dimensions={2,4,6}, to_apply=%region_0.0 | reduce | flops 114688 | bytes 589828 | tf_op jit(solution)/shard_map/reduce_sum | solution.py:40
  99.1 4.6 collective-permute-start.14
  116.8 4.3 collective-permute-done.18
  122.5 4.7 collective-permute-start.20
  147.5 4.4 collective-permute-start.26
  153.9 4.4 collective-permute-done.27
  167.8 47.4 %all-gather.1 = f32[64,2,16]{2,1,0:T(2,128)S(1)} all-gather(f32[2,2,16]{2,1,0:T(2,128)S(1)} %multiply_add_fusion.3), channel_id=3, replica_groups=mesh['gx'=2,'gy'=4,'gz'=4] {'gx','gy','gz'}, dimensions={0}, use_global_device_ids=true | all-gather | bytes 8448 | tf_op jit(solution)/shard_map/all_gather | solution.py:108
  230.3 40.5 %all-gather = f32[128,2,2,16]{3,2,1,0:T(2,128)S(1)} all-gather(f32[4,2,2,16]{3,2,1,0:T(2,128)S(1)} %copy.1905), channel_id=2, replica_groups=mesh['gx'=2,'gy'=4,'gz'=4] {'gx','gy','gz'}, dimensions={0}, use_global_device_ids=true | all-gather | bytes 33792 | tf_op jit(solution)/shard_map/all_gather | solution.py:115
  283.1 4.3 collective-permute-done.39
  298.2 4.3 collective-permute-done.42
  305.7 4.3 collective-permute-done.45
  327.9 4.6 collective-permute-start.50
  336.8 4.6 collective-permute-start.53
  351.6 4.7 collective-permute-start.56
  360.7 5.0 collective-permute-start.59
  369.2 7.8 broadcast_in_dim.14
  377.0 10.0 copy.1931
  397.4 4.7 collective-permute-start.62
  404.8 4.3 collective-permute-start.65
  410.5 5.8 collective-permute-done.64
  427.3 4.8 collective-permute-start.68
  453.3 4.8 collective-permute-start.74
  469.4 41.7 %all-reduce.14 = (f32[4]{0:T(128)S(1)}, f32[4]{0:T(128)S(1)}) all-reduce(f32[4]{0:T(128)S(1)} %get-tuple-element.13, f32[4]{0:T(128)S(1)} %get-tuple-element.12), channel_id=1, replica_groups=mesh['gx'=2,'gy'=4,'gz'=4] {'gx','gy','gz'}, use_global_device_ids=true, to_apply=%region_7.8 | all-reduce | flops 8 | bytes 64 | tf_op jit(solution)/shard_map/psum | solution.py:154
  524.1 4.5 collective-permute-start.80
  549.7 4.8 collective-permute-start.86
  566.6 8.8 copy.1982
  575.4 13.1 %reduce_sum.134 = f32[4,8,8,64]{0,3,2,1:T(8,128)} reduce(f32[4,8,2,8,2,64,2]{0,6,5,4,3,2,1:T(2,128)} %bitcast.23, f32[]{:T(128)} %constant.28.clone.1), dimensions={2,4,6}, to_apply=%region_10.11 | reduce | flops 114688 | bytes 589828 | tf_op jit(solution)/shard_map/reduce_sum | solution.py:40
  599.5 4.9 collective-permute-start.92
  623.1 4.7 collective-permute-start.98
  651.7 4.4 collective-permute-start.104
  658.0 4.4 collective-permute-done.105
  701.5 44.2 %all-gather.2 = f32[128,2,2,16]{3,2,1,0:T(2,128)S(1)} all-gather(f32[4,2,2,16]{3,2,1,0:T(2,128)S(1)} %copy.2005), channel_id=4, replica_groups=mesh['gx'=2,'gy'=4,'gz'=4] {'gx','gy','gz'}, dimensions={0}, use_global_device_ids=true | all-gather | bytes 33792 | tf_op jit(solution)/shard_map/all_gather | solution.py:115
  814.7 4.6 collective-permute-start.128
  836.6 5.0 collective-permute-start.134
  853.4 8.9 broadcast_in_dim.17
  862.3 10.0 copy.2029
  882.7 5.0 collective-permute-start.140
  893.6 5.8 collective-permute-done.142
  910.4 5.1 collective-permute-start.146
  926.6 41.6 %psum.37 = f32[4]{0:T(128)S(1)} all-reduce(f32[4]{0:T(128)S(1)} %get-tuple-element.18), channel_id=1, replica_groups=mesh['gx'=2,'gy'=4,'gz'=4] {'gx','gy','gz'}, use_global_device_ids=true, to_apply=%region_14.15 | all-reduce | flops 4 | bytes 32 | tf_op jit(solution)/shard_map/psum | solution.py:154
  980.9 4.5 collective-permute-start.152
  995.8 41.6 %psum.38 = f32[4]{0:T(128)S(1)} all-reduce(f32[4]{0:T(128)S(1)} %get-tuple-element.16), channel_id=1, replica_groups=mesh['gx'=2,'gy'=4,'gz'=4] {'gx','gy','gz'}, use_global_device_ids=true, to_apply=%region_16.17 | all-reduce | flops 4 | bytes 32 | tf_op jit(solution)/shard_map/psum | solution.py:161
  1038.5 41.2 %psum.39 = f32[4]{0:T(128)S(1)} all-reduce(f32[4]{0:T(128)S(1)} %get-tuple-element.199), channel_id=1, replica_groups=mesh['gx'=2,'gy'=4,'gz'=4] {'gx','gy','gz'}, use_global_device_ids=true, to_apply=%region_18.19 | all-reduce | flops 4 | bytes 32 | tf_op jit(solution)/shard_map/psum | solution.py:169
  (671 shorter events, 538.8 us)
Async XLA Ops:
  2.7 6.5 collective-permute-start.1
  14.2 6.3 collective-permute-start.3
  38.6 20.4 %collective-permute-start.9 = (f32[4,18,16,1]{1,2,3,0:T(8,128)S(1)}, f32[4,18,16,1]{1,2,3,0:T(8,128)S(1)}, u32[]{:S(2)}, u32[]{:S(2)}) collective-permute-start(f32[4,18,16,1]{1,2,3,0:T(8,128)S(1)} %copy.1873), channel_id=1, source_target_pairs={{4,0},{8,4},{12,8},{5,1},{9,5},{13,9},{6,2},{10,6},{14,10},{7,3},{... | collective-permute-start | bytes 13832 | tf_op jit(solution)/shard_map/ppermute | solution.py:22
  40.4 19.1 %collective-permute-start.8 = (f32[4,18,16,1]{1,2,3,0:T(8,128)S(1)}, f32[4,18,16,1]{1,2,3,0:T(8,128)S(1)}, u32[]{:S(2)}, u32[]{:S(2)}) collective-permute-start(f32[4,18,16,1]{1,2,3,0:T(8,128)S(1)} %copy.1872), channel_id=1, source_target_pairs={{0,4},{4,8},{8,12},{1,5},{5,9},{9,13},{2,6},{6,10},{10,14},{3,7},{... | collective-permute-start | bytes 13832 | tf_op jit(solution)/shard_map/ppermute | solution.py:19
  97.8 8.1 collective-permute-start.15
  99.1 8.5 collective-permute-start.14
  121.2 8.8 collective-permute-start.21
  122.5 8.7 collective-permute-start.20
  147.5 6.3 collective-permute-start.26
  151.9 6.3 collective-permute-start.27
  164.9 50.5 %collective-permute-start.31 = (f32[4,1,4,32]{0,3,2,1:T(8,128)S(1)}, f32[4,1,4,32]{0,3,2,1:T(8,128)S(1)}, u32[]{:S(2)}, u32[]{:S(2)}) collective-permute-start(f32[4,1,4,32]{0,3,2,1:T(8,128)S(1)} %get-tuple-element.127), channel_id=1, source_target_pairs={{0,16},{1,17},{2,18},{3,19},{4,20},{5,21},{6,22},{7,23},{8,24},{9,... | collective-permute-start | bytes 6152 | tf_op jit(solution)/shard_map/ppermute | solution.py:19
  166.5 49.0 %collective-permute-start.30 = (f32[4,1,4,32]{0,3,2,1:T(8,128)S(1)}, f32[4,1,4,32]{0,3,2,1:T(8,128)S(1)}, u32[]{:S(2)}, u32[]{:S(2)}) collective-permute-start(f32[4,1,4,32]{0,3,2,1:T(8,128)S(1)} %get-tuple-element.128), channel_id=1, source_target_pairs={{16,0},{17,1},{18,2},{19,3},{20,4},{21,5},{22,6},{23,7},{24,8},{25... | collective-permute-start | bytes 6152 | tf_op jit(solution)/shard_map/ppermute | solution.py:22
  295.7 6.7 collective-permute-start.42
  326.6 7.2 collective-permute-start.51
  327.9 7.4 collective-permute-start.50
  350.3 7.4 collective-permute-start.57
  351.6 7.5 collective-permute-start.56
  359.4 6.3 collective-permute-start.58
  395.6 6.5 collective-permute-start.63
  397.4 6.3 collective-permute-start.62
  409.1 7.2 collective-permute-start.64
  425.5 6.6 collective-permute-start.69
  427.3 6.4 collective-permute-start.68
  451.5 6.6 collective-permute-start.75
  453.3 6.4 collective-permute-start.74
  522.3 6.3 collective-permute-start.81
  548.0 6.6 collective-permute-start.87
  549.7 6.4 collective-permute-start.86
  598.2 8.4 collective-permute-start.93
  599.5 8.8 collective-permute-start.92
  621.8 8.8 collective-permute-start.99
  623.1 8.7 collective-permute-start.98
  651.7 6.3 collective-permute-start.104
  656.1 6.3 collective-permute-start.105
  663.6 6.9 collective-permute-start.106
  766.0 7.1 collective-permute-start.118
  767.3 6.4 collective-permute-start.119
  792.4 6.9 collective-permute-start.124
  813.4 7.2 collective-permute-start.129
  814.7 7.4 collective-permute-start.128
  835.3 9.0 collective-permute-start.135
  836.6 8.9 collective-permute-start.134
  880.9 6.8 collective-permute-start.141
  882.7 6.6 collective-permute-start.140
  892.2 7.2 collective-permute-start.142
  908.7 6.9 collective-permute-start.147
  910.4 6.4 collective-permute-start.146
  979.1 6.3 collective-permute-start.153
  (128 other events, 820.1 us)
where the time goes:
time: 1090 us; the launch traced here: 1080 us
  starting transfers between devices  340 us (31%)
  blocking collectives  298 us (27%)
  waiting for transfers between devices  234 us (21%)
  local copies, waits for them, and re-layouts  131 us (12%)
  other arithmetic  74.1 us (7%)
    ppermute x78, starting transfers between devices, extended(): lax.ppermute(lax.slice_in_dim(block, block.shape[dim] - width, None, axis...  238 us
    ppermute x78, waiting for transfers between devices, extended(): lax.ppermute(lax.slice_in_dim(block, 0, width, axis=dim), axis, backward)  195 us
    ppermute x78, starting transfers between devices, extended(): lax.ppermute(lax.slice_in_dim(block, 0, width, axis=dim), axis, backward)  101 us
    all_gather x2, blocking collectives, coarsest(): lax.all_gather(rhs_field[None], ('gx', 'gy', 'gz'), axis=0, tiled=True)  84.7 us
    psum x2, blocking collectives, precond_sum(): return lax.psum(local_dot(first_field, second_field), ('gx', 'gy', 'gz'))  83.3 us
    all_gather x1, blocking collectives, per_device(): lax.all_gather(diagonals[LEVELS][None], ('gx', 'gy', 'gz'), axis=0, tiled...  47.4 us
    psum x1, blocking collectives, per_device(): lax.psum(local_dot(search, operated), ('gx', 'gy', 'gz'))  41.6 us
    psum x1, blocking collectives, per_device(): squares = lax.psum(local_dot(residual, residual), ('gx', 'gy', 'gz'))  41.2 us
  transfers between devices with their start and end apart: 156, of which 110 were waited for; matrix products, arithmetic and copies ran while one was open for 3% of the time, Pallas kernels for 0%

commit v1 on v0

v1 whole, which is shorter than its diff:
```python
import functools
import math

import jax
import jax.numpy as jnp
from jax import lax
from jax.experimental import pallas as pl
from jax.experimental.pallas import tpu as pltpu
from jax.sharding import PartitionSpec as P

LEVELS = 3
COARSE_SWEEPS = 8
DAMP = 0.8
LANES = 128
F32 = jnp.float32
MESH = pl.DeviceIdType.MESH
AXES = ("gx", "gz", "gy")


def dot(a, b):
    return jnp.dot(a, b, precision=lax.Precision.HIGHEST, preferred_element_type=F32)


def body(cfg, kappa, bits, x_out, rel_out, *scr):
    probes, sizes, counts, reach, width = cfg
    nx, nz, ny = counts["gx"], counts["gz"], counts["gy"]
    total = nx * nz * ny
    (v0, b0, r0, p0, q0, d0, w0, v1, b1, d1, w1,
     xr0, zs0, zr0, ys0, yr0, xr1, zs1, zr1, ys1, yr1, ss, rs,
     tmp, gsend, gk, gr, gss, gks, grs, v2, b2, k2, w2, b3, d2, k3, e3,
     asend, arecv, ass, ars) = scr
    xr, zs, zr, ys, yr = (xr0, xr1), (zs0, zs1), (zr0, zr1), (ys0, ys1), (yr0, yr1)
    me = {a: lax.axis_index(a) for a in AXES}
    coup = [0.25**l for l in range(LEVELS + 1)]

    def iota(shape, dim):
        return lax.broadcasted_iota(jnp.int32, shape, dim)

    def zero(ref):
        ref[...] = jnp.zeros(ref.shape, F32)

    ri, ci = iota((LANES, LANES), 0), iota((LANES, LANES), 1)
    pool_m = jnp.where(ri // 2 == ci, 0.125, 0.0).astype(F32)
    spread_m = jnp.where(ci // 2 == ri, 1.0, 0.0).astype(F32)
    y2 = sizes[2][2]
    own_m = jnp.where((ci // 2 + reach * y2 == ri) & (ci < 2 * y2), 1.0, 0.0).astype(F32)

    def pool(f):
        cx, cz, _ = f.shape
        s = f.reshape(cx // 2, 2, cz, LANES)
        s = (s[:, 0] + s[:, 1]).reshape(cx // 2 * cz, LANES)
        rows = cx // 2 * cz
        tmp[pl.ds(0, rows), :] = s
        h = tmp[pl.ds(0, rows // 2, stride=2), :] + tmp[pl.ds(1, rows // 2, stride=2), :]
        return dot(h, pool_m)

    def spread(e, cx, cz, mat):
        rows = cx * cz
        f = dot(e, mat)
        tmp[pl.ds(0, rows, stride=2), :] = f
        tmp[pl.ds(1, rows, stride=2), :] = f
        g = tmp[pl.ds(0, 2 * rows), :].reshape(cx, 1, 2 * cz, LANES)
        return jnp.broadcast_to(g, (cx, 2, 2 * cz, LANES)).reshape(2 * cx, 2 * cz, LANES)

    def face_copies(level, par, field):
        X = sizes[level][0]
        out = []
        for ai, axis in enumerate(AXES):
            for side in (0, 1):
                if ai == 0:
                    src = field.at[:, 0 if side == 0 else X - 1]
                    dst = xr[level].at[par, 1 - side]
                elif ai == 1:
                    src, dst = zs[level].at[par, side], zr[level].at[par, 1 - side]
                else:
                    src, dst = ys[level].at[par, side], yr[level].at[par, 1 - side]
                step = -1 if side == 0 else 1
                ok = me[axis] > 0 if side == 0 else me[axis] < counts[axis] - 1

                def make(src=src, dst=dst, ai=ai, side=side, axis=axis, step=step, flip=False):
                    return pltpu.make_async_remote_copy(
                        src_ref=src, dst_ref=dst,
                        send_sem=ss.at[level, par, ai, side],
                        recv_sem=rs.at[level, par, ai, side if flip else 1 - side],
                        device_id={axis: me[axis] + step}, device_id_type=MESH)

                out.append((ok, make))
        return out

    def start(level, par, field):
        for ok, make in face_copies(level, par, field):
            @pl.when(ok)
            def _(make=make):
                make().start()

    def finish(level, par, field):
        for ok, make in face_copies(level, par, field):
            @pl.when(ok)
            def _(make=make):
                make(flip=True).wait_recv()
                make().wait_send()

    def pack(level, par, v, p):
        X, Z, Y = sizes[level]
        zs[level][par, 0, p] = v[:, 0:1, :]
        zs[level][par, 1, p] = v[:, Z - 1 : Z, :]
        lane = iota((Z, LANES), 1)
        lo = v[0]
        hi = pltpu.roll(v[0], (LANES - (Y - 1)) % LANES, 1)
        for x in range(1, X):
            lo = jnp.where(lane == x, pltpu.roll(v[x], x, 1), lo)
            hi = jnp.where(lane == x, pltpu.roll(v[x], (x - (Y - 1)) % LANES, 1), hi)
        mine = (lane >= p * X) & (lane < p * X + X)
        ys[level][par, 0] = jnp.where(mine, pltpu.roll(lo, p * X, 1), ys[level][par, 0])
        ys[level][par, 1] = jnp.where(mine, pltpu.roll(hi, p * X, 1), ys[level][par, 1])

    def near(level, par, v, p):
        X, Z, Y = sizes[level]
        sub, lane = iota((X, Z, LANES), 1), iota((X, Z, LANES), 2)
        n = jnp.concatenate([xr[level][par, 0, p][None], v[:-1]], 0)
        n = n + jnp.concatenate([v[1:], xr[level][par, 1, p][None]], 0)
        n = n + jnp.where(sub == 0, zr[level][par, 0, p], pltpu.roll(v, 1, 1))
        n = n + jnp.where(sub == Z - 1, zr[level][par, 1, p], pltpu.roll(v, Z - 1, 1))
        back = lax.rem(LANES - p * X, LANES)
        lo = pltpu.roll(yr[level][par, 0], back, 1)
        hi = pltpu.roll(yr[level][par, 1], back, 1)
        los = jnp.stack([pltpu.roll(lo, (LANES - x) % LANES, 1) for x in range(X)], 0)
        his = jnp.stack([pltpu.roll(hi, (Y - 1 - x) % LANES, 1) for x in range(X)], 0)
        n = n + jnp.where(lane == 0, los, pltpu.roll(v, 1, 2))
        n = n + jnp.where(lane == Y - 1, his, pltpu.roll(v, LANES - 1, 2))
        return n

    def flat_near(v, Y):
        X, Z, _ = v.shape
        sub, lane = iota(v.shape, 1), iota(v.shape, 2)
        none = jnp.zeros((1, Z, LANES), F32)
        n = jnp.concatenate([none, v[:-1]], 0) + jnp.concatenate([v[1:], none], 0)
        n = n + jnp.where(sub == 0, 0.0, pltpu.roll(v, 1, 1))
        n = n + jnp.where(sub == Z - 1, 0.0, pltpu.roll(v, Z - 1, 1))
        n = n + jnp.where(lane == 0, 0.0, pltpu.roll(v, 1, 2))
        n = n + jnp.where(lane >= Y - 1, 0.0, pltpu.roll(v, LANES - 1, 2))
        return n

    def per_probe(fn):
        def step(p, c):
            fn(p)
            return c
        lax.fori_loop(0, probes, step, 0)

    steps = [0, 0]

    def exchange(level, field):
        par = steps[level] % 2
        steps[level] += 1
        start(level, par, field)
        finish(level, par, field)
        return par

    Xc, Zc, Yc = sizes[2]
    rows2 = Xc * Zc

    def gather_copies(dst_ref, sems, which):
        out = []
        for a in range(nx):
            for c in range(nz):
                for o in range(width):
                    if (a, c, o) == (0, 0, reach):
                        continue
                    tx, tz = lax.rem(me["gx"] + a, nx), lax.rem(me["gz"] + c, nz)
                    ty = me["gy"] + (reach - o)
                    slot = (me["gx"] * nz + me["gz"]) * width + o
                    fx, fz = lax.rem(me["gx"] + nx - a, nx), lax.rem(me["gz"] + nz - c, nz)
                    fslot = (fx * nz + fz) * width + o
                    fy = me["gy"] + (o - reach)
                    sidx = (a * nz + c) * width + o

                    def make(tx=tx, tz=tz, ty=ty, slot=slot, sidx=sidx):
                        return pltpu.make_async_remote_copy(
                            src_ref=gsend.at[which], dst_ref=dst_ref.at[slot],
                            send_sem=gss.at[which, sidx], recv_sem=sems.at[slot],
                            device_id={"gx": tx, "gz": tz, "gy": ty}, device_id_type=MESH)

                    def take(tx=tx, tz=tz, ty=ty, fslot=fslot, sidx=sidx):
                        return pltpu.make_async_remote_copy(
                            src_ref=gsend.at[which], dst_ref=dst_ref.at[fslot],
                            send_sem=gss.at[which, sidx], recv_sem=sems.at[fslot],
                            device_id={"gx": tx, "gz": tz, "gy": ty}, device_id_type=MESH)

                    out.append(((ty >= 0) & (ty < ny), make, (fy >= 0) & (fy < ny), take))
        return out

    def gather_start(dst_ref, sems, which):
        for ok, make, _, _ in gather_copies(dst_ref, sems, which):
            @pl.when(ok)
            def _(make=make):
                make().start()
        dst_ref[(me["gx"] * nz + me["gz"]) * width + reach] = gsend[which]

    def gather_finish(dst_ref, sems, which):
        for ok, make, okr, take in gather_copies(dst_ref, sems, which):
            @pl.when(okr)
            def _(take=take):
                take().wait_recv()

            @pl.when(ok)
            def _(make=make):
                make().wait_send()

    def gather_clear(dst_ref):
        for o in range(width):
            fy = me["gy"] + (o - reach)

            @pl.when((fy < 0) | (fy >= ny))
            def _(o=o):
                for s in range(nx * nz):
                    dst_ref[s * width + o] = jnp.zeros((rows2, LANES), F32)

    def unpack(src_ref, out_ref, lead):
        lane = iota((rows2, LANES), 1)
        for sx in range(nx):
            for sz in range(nz):
                tiles = [src_ref[(sx * nz + sz) * width + o] for o in range(width)]
                for p in range(lead):
                    t = jnp.zeros((rows2, LANES), F32)
                    for o in range(width):
                        t = jnp.where(lane // Yc == o, pltpu.roll(tiles[o], ((o - p) * Yc) % LANES, 1), t)
                    for x in range(Xc):
                        out_ref[p, sx * Xc + x, pl.ds(sz * Zc, Zc), :] = t[x * Zc : (x + 1) * Zc]

    def slot_of(x, z, y):
        return (x * nz + z) * ny + y

    def reduce_copies(which, mine_slot):
        out = []
        for a in range(nx):
            for c in range(nz):
                for o in range(ny):
                    if (a, c, o) == (0, 0, 0):
                        continue
                    t = {"gx": lax.rem(me["gx"] + a, nx), "gz": lax.rem(me["gz"] + c, nz),
                         "gy": lax.rem(me["gy"] + o, ny)}
                    f = slot_of(lax.rem(me["gx"] + nx - a, nx), lax.rem(me["gz"] + nz - c, nz),
                                lax.rem(me["gy"] + ny - o, ny))
                    slot = f if not mine_slot else slot_of(me["gx"], me["gz"], me["gy"])
                    out.append(pltpu.make_async_remote_copy(
                        src_ref=asend.at[which], dst_ref=arecv.at[which, slot],
                        send_sem=ass.at[which, slot_of(a, c, o)], recv_sem=ars.at[which, slot],
                        device_id=t, device_id_type=MESH))
        return out

    def reduce_start(which, row):
        asend[which] = row
        for cp in reduce_copies(which, True):
            cp.start()
        arecv[which, slot_of(me["gx"], me["gz"], me["gy"])] = row

    def reduce_finish(which):
        for cp in reduce_copies(which, False):
            cp.wait_recv()
            cp.wait_send()
        return jnp.sum(arecv[which], axis=0)

    lane1 = iota((1, LANES), 1)

    def whole(f):
        s = jnp.sum(f, axis=0)
        return jnp.sum(jnp.sum(s, axis=0, keepdims=True), axis=1, keepdims=True)

    def put(row, q, p, f):
        return jnp.where(lane1 == q * probes + p, whole(f), row)

    def get(row, q, p):
        return jnp.sum(jnp.where(lane1 == q * probes + p, row, 0.0), axis=1, keepdims=True)

    for level in (0, 1):
        for ai, axis in enumerate(AXES):
            for side in (0, 1):
                @pl.when(me[axis] == (0 if side == 0 else counts[axis] - 1))
                def _(level=level, ai=ai, side=side):
                    ref = (xr, zr, yr)[ai][level]
                    for par in (0, 1):
                        ref[par, side] = jnp.zeros(ref.shape[2:], F32)
        zero(ys[level])
    gather_clear(gk)
    for i in (0, 1):
        gather_clear(gr.at[i])

    X0, Z0, Y0 = sizes[0]
    X1, Z1, Y1 = sizes[1]
    k0 = kappa[...]
    d0[...] = k0 + 6.0
    w0[...] = DAMP / d0[...]
    k1 = pool(k0).reshape(X1, Z1, LANES)
    lv1 = iota((X1, Z1, LANES), 2) < Y1
    dd1 = k1 + 6.0 * coup[1]
    d1[...] = dd1
    w1[...] = jnp.where(lv1, DAMP / dd1, 0.0)
    gsend[2] = pool(k1)
    gather_start(gk, gks, 2)

    def first(rhs):
        par = steps[0] % 2

        def fn(p):
            v = w0[...] * rhs[p]
            v0[p] = v
            pack(0, par, v, p)
        return fn

    XG, ZG = nx * Xc, nz * Zc
    WY = width * Yc

    def coefs2():
        gather_finish(gk, gks, 2)
        unpack(gk, k2, 1)
        kk = k2[0]
        lane = iota(kk.shape, 2)
        gy0 = lane + (me["gy"] - reach) * Yc
        ok = (lane < WY) & (gy0 >= 0) & (gy0 < ny * Yc)
        dd = kk + 6.0 * coup[2]
        d2[...] = dd
        w2[...] = jnp.where(ok, DAMP / dd, 0.0)
        c3 = pool(kk).reshape(XG // 2, ZG // 2, LANES)
        lane = iota(c3.shape, 2)
        gy0 = lane + (me["gy"] - reach) * (Yc // 2)
        ok = (lane < WY // 2) & (gy0 >= 0) & (gy0 < ny * (Yc // 2))
        k3[...] = jnp.where(ok, DAMP / (c3 + 6.0 * coup[3]), 0.0)

    def coarse_part(which):
        src = gr.at[which]
        unpack(src, b2, probes)

        def fn(p):
            b = b2[p]
            w = w2[...]
            v = w * b
            v = (1.0 - DAMP) * v + w * (b + coup[2] * flat_near(v, WY))
            r = b - d2[...] * v + coup[2] * flat_near(v, WY)
            r = jnp.where(w > 0.0, r, 0.0)
            c = pool(r).reshape(XG // 2, ZG // 2, LANES)
            w3 = k3[...]
            u = w3 * c
            for _ in range(COARSE_SWEEPS - 1):
                u = (1.0 - DAMP) * u + w3 * (c + coup[3] * flat_near(u, WY // 2))
            e = spread(u.reshape(XG // 2 * (ZG // 2), LANES), XG // 2, ZG // 2, spread_m)
            v = v + jnp.where(w > 0.0, e, 0.0)
            for _ in range(2):
                v = (1.0 - DAMP) * v + w * (b + coup[2] * flat_near(v, WY))
            v2[p] = v
        per_probe(fn)

    def sweep(level, rhs, field, more=True):
        par = exchange(level, field)
        d, w = (d0, d1)[level], (w0, w1)[level]
        nxt = steps[level] % 2

        def fn(p):
            v = field[p]
            v = (1.0 - DAMP) * v + w[...] * (rhs[p] + coup[level] * near(level, par, v, p))
            field[p] = v
            if more:
                pack(level, nxt, v, p)
        per_probe(fn)

    def vcycle(rhs, which):
        per_probe(first(rhs))
        sweep(0, rhs, v0)
        par = exchange(0, v0)
        par1 = steps[1] % 2

        def down(p, par=par):
            v = v0[p]
            r = rhs[p] - d0[...] * v + near(0, par, v, p)
            b = pool(r).reshape(X1, Z1, LANES)
            b1[p] = b
            v = w1[...] * b
            v1[p] = v
            pack(1, par1, v, p)
        per_probe(down)
        sweep(1, b1, v1)
        par = exchange(1, v1)
        gsend[which] = jnp.zeros((rows2, LANES), F32)

        def down1(p, par=par):
            v = v1[p]
            r = b1[p] - d1[...] * v + coup[1] * near(1, par, v, p)
            r = jnp.where(lv1, r, 0.0)
            gsend[which] = gsend[which] + pltpu.roll(pool(r), p * Yc, 1)
        per_probe(down1)
        gather_start(gr.at[which], grs.at[which], which)
        if which == 0:
            coefs2()
        gather_finish(gr.at[which], grs.at[which], which)
        coarse_part(which)
        nxt = steps[1] % 2

        def up1(p):
            for x in range(Xc):
                e3[pl.ds(x * Zc, Zc), :] = v2[p, me["gx"] * Xc + x, pl.ds(me["gz"] * Zc, Zc), :]
            v = v1[p] + spread(e3[...], Xc, Zc, own_m)
            v1[p] = v
            pack(1, nxt, v, p)
        per_probe(up1)
        sweep(1, b1, v1)
        sweep(1, b1, v1, more=False)
        nxt0 = steps[0] % 2

        def up0(p):
            v = v0[p] + spread(v1[p].reshape(X1 * Z1, LANES), X1, Z1, spread_m)
            v0[p] = v
            pack(0, nxt0, v, p)
        per_probe(up0)
        sweep(0, rhs, v0)
        sweep(0, rhs, v0)

    def begin(p):
        r0[p] = 2.0 * bits[p].astype(F32) - 1.0
    per_probe(begin)
    vcycle(r0, 0)
    par = exchange(0, v0)

    def image(p, row, par=par):
        v = v0[p]
        q = d0[...] * v - near(0, par, v, p)
        p0[p] = v
        q0[p] = q
        row = put(row, 0, p, r0[p] * v)
        return put(row, 1, p, v * q)
    row = lax.fori_loop(0, probes, image, jnp.zeros((1, LANES), F32))
    reduce_start(0, row)
    vcycle(q0, 1)
    sums0 = reduce_finish(0)
    nxt = steps[0] % 2

    def direction(p):
        a = get(sums0, 0, p) / get(sums0, 1, p)
        v = p0[p] - a * v0[p]
        v0[p] = v
        r0[p] = r0[p] - a * q0[p]
        pack(0, nxt, v, p)
    per_probe(direction)
    par = exchange(0, v0)

    def image2(p, row, par=par):
        v = v0[p]
        t = d0[...] * v - near(0, par, v, p)
        b0[p] = t
        row = put(row, 0, p, r0[p] * v)
        row = put(row, 1, p, v * t)
        return put(row, 2, p, v * q0[p])
    row = lax.fori_loop(0, probes, image2, jnp.zeros((1, LANES), F32))
    reduce_start(1, row)
    sums1 = reduce_finish(1)

    def final(p, row):
        rz0, pq0 = get(sums0, 0, p), get(sums0, 1, p)
        rz1, pt, pq = get(sums1, 0, p), get(sums1, 1, p), get(sums1, 2, p)
        a0 = rz0 / pq0
        beta = rz1 / rz0
        a1 = rz1 / (pt + 2.0 * beta * pq + beta * beta * pq0)
        x_out[p] = a0 * p0[p] + a1 * (v0[p] + beta * p0[p])
        r = r0[p] - a1 * (b0[p] + beta * q0[p])
        return put(row, 0, p, r * r)
    row = lax.fori_loop(0, probes, final, jnp.zeros((1, LANES), F32))
    reduce_start(2, row)
    cells = float(X0 * Z0 * Y0 * total)
    rel_out[...] = jnp.sqrt(reduce_finish(2) / cells)


def per_device(mesh_counts, kappa_sq, probe_bits):
    probes, X, Z, Y = probe_bits.shape
    sizes = [(X >> l, Z >> l, Y >> l) for l in range(LEVELS + 1)]
    need = 2 * (1 + COARSE_SWEEPS - 1) + 2
    reach = min(math.ceil(need / sizes[2][2]), mesh_counts["gy"] - 1)
    width = 2 * reach + 1
    assert Y <= LANES and width * sizes[2][2] <= LANES and probes * X <= LANES
    assert probes * sizes[2][2] <= LANES
    nx, nz, ny = mesh_counts["gx"], mesh_counts["gz"], mesh_counts["gy"]
    total = nx * nz * ny
    slots = nx * nz * width
    Xc, Zc, Yc = sizes[2]
    XG, ZG = nx * Xc, nz * Zc

    def vm(*shape):
        return pltpu.VMEM(shape, F32)

    def full(level):
        return vm(probes, sizes[level][0], sizes[level][1], LANES)

    def coef(level):
        return vm(sizes[level][0], sizes[level][1], LANES)

    def halo(level):
        x, z, _ = sizes[level]
        return [vm(2, 2, probes, z, LANES), vm(2, 2, probes, x, 1, LANES),
                vm(2, 2, probes, x, 1, LANES), vm(2, 2, z, LANES), vm(2, 2, z, LANES)]

    dma = pltpu.SemaphoreType.DMA
    scratch = [full(0), full(0), full(0), full(0), full(0), coef(0), coef(0),
               full(1), full(1), coef(1), coef(1), *halo(0), *halo(1),
               dma((2, 2, 3, 2)), dma((2, 2, 3, 2)),
               vm(max(X * Z, XG * ZG), LANES), vm(3, Xc * Zc, LANES),
               vm(slots, Xc * Zc, LANES), vm(2, slots, Xc * Zc, LANES),
               dma((3, slots)), dma((slots,)), dma((2, slots)),
               vm(probes, XG, ZG, LANES), vm(probes, XG, ZG, LANES), vm(1, XG, ZG, LANES),
               vm(XG, ZG, LANES), vm(probes, XG // 2, ZG // 2, LANES), vm(XG, ZG, LANES),
               vm(XG // 2, ZG // 2, LANES), vm(Xc * Zc, LANES),
               vm(3, 1, LANES), vm(3, total, 1, LANES), dma((3, total)), dma((3, total))]
    cfg = (probes, sizes, mesh_counts, reach, width)
    field, rel = pl.pallas_call(
        functools.partial(body, cfg),
        out_shape=(jax.ShapeDtypeStruct(probe_bits.shape, F32),
                   jax.ShapeDtypeStruct((1, LANES), F32)),
        in_specs=[pl.BlockSpec(memory_space=pltpu.VMEM)] * 2,
        out_specs=(pl.BlockSpec(memory_space=pltpu.VMEM),) * 2,
        scratch_shapes=scratch,
        compiler_params=pltpu.CompilerParams(has_side_effects=True, vmem_limit_bytes=48 * 2**20),
    )(kappa_sq, probe_bits)
    return field, rel[0, :probes]


def solution(mesh):
    return jax.shard_map(
        functools.partial(per_device, dict(mesh.shape)),
        mesh=mesh,
        in_specs=(P("gx", "gz", "gy"), P(None, "gx", "gz", "gy")),
        out_specs=(P(None, "gx", "gz", "gy"), P()),
        check_vma=False,
    )
```

time: 1090 us -> 134 us (0.12)
  starting transfers between devices: 340 us -> 0 us
  blocking collectives: 298 us -> 0 us
  waiting for transfers between devices: 234 us -> 0 us
  Pallas kernels: 0 us -> 130 us
  local copies, waits for them, and re-layouts: 131 us -> 3.24 us
  other arithmetic: 74.1 us -> 0 us
    ppermute x156 -> x0, starting transfers between devices: 340 us -> none  [the longest x78 238 us: extended(): lax.ppermute(lax.slice_in_dim(block, block.shape[dim] - width, None, axis...]
    ppermute x156 -> x0, waiting for transfers between devices: 234 us -> none  [the longest x78 195 us: extended(): lax.ppermute(lax.slice_in_dim(block, 0, width, axis=dim), axis, backward)]
    psum x4 -> x0, blocking collectives: 166 us -> none  [the longest x2 83.3 us: precond_sum(): return lax.psum(local_dot(first_field, second_field), ('gx', 'gy', 'gz'))]
    all_gather x3 -> x0, blocking collectives: 132 us -> none  [the longest x2 84.7 us: coarsest(): lax.all_gather(rhs_field[None], ('gx', 'gy', 'gz'), axis=0, tiled=True)]
    pallas_call x0 -> x1, Pallas kernels: none -> 130 us  [per_device(): pl.pallas_call(functools.partial(body, cfg), out_shape=(jax.ShapeDtypeStr...]
    reduce_sum x13 -> x0, other arithmetic: 38.7 us -> none  [the longest x9 34.7 us: coarsen(): return jnp.mean(grouped, axis=(-5, -3, -1))]
    reshape x7 -> x0, local copies, waits for them, and re-layouts: 33.7 us -> none  [the longest x4 23.6 us: refine(): spread.reshape(leading + (cells_first * 2, cells_second * 2, cells_third...]
    sub x4 -> x0, local copies, waits for them, and re-layouts: 20.4 us -> none  [vcycle(): remainder = rhs_field - operate(field, diagonal, coupling, grid_level)]
  transfers between devices with their start and end apart: 156 -> 0, of which waited for: 110 -> 0; matrix products, arithmetic and copies ran while one was open for 3% -> 0% of each run, Pallas kernels for 0% -> 0%
where the time goes in v1:
time: 134 us
  Pallas kernels  130 us (97%)
  local copies, waits for them, and re-layouts  3.24 us (2%)
    pallas_call x1, Pallas kernels, per_device(): pl.pallas_call(functools.partial(body, cfg), out_shape=(jax.ShapeDtypeStr...  130 us
    unnamed x5, local copies, waits for them, and re-layouts  2.73 us

profile of v1, /device:TPU:0, one launch (start us, length us, event | category | flops | bytes accessed | tf_op | source)
XLA Modules:
  0.0 134.3 jit_solution(15609243055978530701)
XLA Ops:
  0.6 0.0 copy-start
  0.6 1.0 copy-done
  1.7 0.0 copy-start.1
  1.7 0.9 copy-done.1
  2.6 130.4 %shard_map.41 = (f32[4,16,16,128]{3,2,1,0:T(8,128)S(1)}, f32[1,128]{1,0:T(1,128)S(1)}) custom-call(f32[16,16,128]{2,1,0:T(8,128)S(1)} %copy-done.1, s32[4,16,16,128]{3,2,1,0:T(8,128)S(1)} %copy-done), custom_call_target="tpu_custom_call" | custom-call | tf_op jit(solution)/shard_map/pallas_call | solution.py:510
  133.0 0.5 slice_bitcast_fusion
  133.5 0.8 copy.5
Async XLA Ops:
  0.6 1.0 copy-start
  1.7 0.9 copy-start.1

commit v2 on v1

--- a/solution.py
+++ b/solution.py
@@ -26,10 +26,11 @@
     nx, nz, ny = counts["gx"], counts["gz"], counts["gy"]
     total = nx * nz * ny
     (v0, b0, r0, p0, q0, d0, w0, v1, b1, d1, w1,
-     xr0, zs0, zr0, ys0, yr0, xr1, zs1, zr1, ys1, yr1, ss, rs,
-     tmp, gsend, gk, gr, gss, gks, grs, v2, b2, k2, w2, b3, d2, k3, e3,
+     xr0, zs0, zr0, ys0, yr0, ym0, xr1, zs1, zr1, ys1, yr1, ym1, ss, rs,
+     tmp, gsend, gk, gr, gss, gks, grs, v2, b2, k2, w2, b3, d2, k3, e3, c3, acc1,
      asend, arecv, ass, ars) = scr
     xr, zs, zr, ys, yr = (xr0, xr1), (zs0, zs1), (zr0, zr1), (ys0, ys1), (yr0, yr1)
+    ym, acc = (ym0, ym1), (b0, acc1)
     me = {a: lax.axis_index(a) for a in AXES}
     coup = [0.25**l for l in range(LEVELS + 1)]
 
@@ -62,10 +63,11 @@
         g = tmp[pl.ds(0, 2 * rows), :].reshape(cx, 1, 2 * cz, LANES)
         return jnp.broadcast_to(g, (cx, 2, 2 * cz, LANES)).reshape(2 * cx, 2 * cz, LANES)
 
-    def face_copies(level, par, field):
+    def face_copies(level, par, field, axes, p=None):
         X = sizes[level][0]
         out = []
-        for ai, axis in enumerate(AXES):
+        for ai in axes:
+            axis = AXES[ai]
             for side in (0, 1):
                 if ai == 0:
                     src = field.at[:, 0 if side == 0 else X - 1]
@@ -73,7 +75,9 @@
                 elif ai == 1:
                     src, dst = zs[level].at[par, side], zr[level].at[par, 1 - side]
                 else:
-                    src, dst = ys[level].at[par, side], yr[level].at[par, 1 - side]
+                    src, dst = ys[level].at[par], yr[level].at[par, 1 - side]
+                if p is not None:
+                    src, dst = src.at[p], dst.at[p]
                 step = -1 if side == 0 else 1
                 ok = me[axis] > 0 if side == 0 else me[axis] < counts[axis] - 1
 
@@ -87,48 +91,60 @@
                 out.append((ok, make))
         return out
 
-    def start(level, par, field):
-        for ok, make in face_copies(level, par, field):
+    def start(level, par, field, axes, p=None):
+        for ok, make in face_copies(level, par, field, axes, p):
             @pl.when(ok)
             def _(make=make):
                 make().start()
 
     def finish(level, par, field):
-        for ok, make in face_copies(level, par, field):
+        for ok, make in face_copies(level, par, field, (0, 1, 2)):
             @pl.when(ok)
             def _(make=make):
                 make(flip=True).wait_recv()
                 make().wait_send()
-
-    def pack(level, par, v, p):
         X, Z, Y = sizes[level]
+        lane = iota((Z, LANES), 1)
+        low = lane % 2 == 1 if Y == LANES else lane < probes * X
+        ym[level][...] = jnp.where(
+            low, pltpu.roll(yr[level][par, 0], LANES - (Y - 1), 1),
+            pltpu.roll(yr[level][par, 1], Y - 1, 1))
+
+    def lane_of(level, p, x):
+        X, _, Y = sizes[level]
+        return 2 * (p * X + x) + 1 if Y == LANES else p * X + x
+
+    def pack(level, par, field, v, p):
+        X, Z, Y = sizes[level]
+        field[p] = v
         zs[level][par, 0, p] = v[:, 0:1, :]
         zs[level][par, 1, p] = v[:, Z - 1 : Z, :]
+        start(level, par, field, (0, 1), p)
         lane = iota((Z, LANES), 1)
-        lo = v[0]
-        hi = pltpu.roll(v[0], (LANES - (Y - 1)) % LANES, 1)
-        for x in range(1, X):
-            lo = jnp.where(lane == x, pltpu.roll(v[x], x, 1), lo)
-            hi = jnp.where(lane == x, pltpu.roll(v[x], (x - (Y - 1)) % LANES, 1), hi)
-        mine = (lane >= p * X) & (lane < p * X + X)
-        ys[level][par, 0] = jnp.where(mine, pltpu.roll(lo, p * X, 1), ys[level][par, 0])
-        ys[level][par, 1] = jnp.where(mine, pltpu.roll(hi, p * X, 1), ys[level][par, 1])
-
-    def near(level, par, v, p):
+        tile = ys[level][par]
+        for x in range(X):
+            s = lane_of(level, p, x)
+            hit = (lane == s) | (lane == lax.rem(s + Y - 1, LANES))
+            tile = jnp.where(hit, pltpu.roll(v[x], s, 1), tile)
+        ys[level][par] = tile
+
+    def halo(level, par, p):
         X, Z, Y = sizes[level]
-        sub, lane = iota((X, Z, LANES), 1), iota((X, Z, LANES), 2)
-        n = jnp.concatenate([xr[level][par, 0, p][None], v[:-1]], 0)
-        n = n + jnp.concatenate([v[1:], xr[level][par, 1, p][None]], 0)
-        n = n + jnp.where(sub == 0, zr[level][par, 0, p], pltpu.roll(v, 1, 1))
-        n = n + jnp.where(sub == Z - 1, zr[level][par, 1, p], pltpu.roll(v, Z - 1, 1))
-        back = lax.rem(LANES - p * X, LANES)
-        lo = pltpu.roll(yr[level][par, 0], back, 1)
-        hi = pltpu.roll(yr[level][par, 1], back, 1)
-        los = jnp.stack([pltpu.roll(lo, (LANES - x) % LANES, 1) for x in range(X)], 0)
-        his = jnp.stack([pltpu.roll(hi, (Y - 1 - x) % LANES, 1) for x in range(X)], 0)
-        n = n + jnp.where(lane == 0, los, pltpu.roll(v, 1, 2))
-        n = n + jnp.where(lane == Y - 1, his, pltpu.roll(v, LANES - 1, 2))
-        return n
+        sub, lane = iota((Z, LANES), 0), iota((Z, LANES), 1)
+        edge = (lane == 0) | (lane == Y - 1)
+        m = ym[level][...]
+        planes = []
+        for x in range(X):
+            back = lax.rem(2 * LANES - lane_of(level, p, x), LANES)
+            h = jnp.where(edge, pltpu.roll(m, back, 1), 0.0)
+            h = h + jnp.where(sub == 0, zr[level][par, 0, p, x],
+                              jnp.where(sub == Z - 1, zr[level][par, 1, p, x], 0.0))
+            if x == 0:
+                h = h + xr[level][par, 0, p]
+            if x == X - 1:
+                h = h + xr[level][par, 1, p]
+            planes.append(h)
+        return jnp.stack(planes, 0)
 
     def flat_near(v, Y):
         X, Z, _ = v.shape
@@ -149,10 +165,15 @@
 
     steps = [0, 0]
 
-    def exchange(level, field):
+    def exchange(level, field, inner):
         par = steps[level] % 2
         steps[level] += 1
-        start(level, par, field)
+        start(level, par, field, (2,))
+
+        def fn(p):
+            v = field[p]
+            acc[level][p] = inner(p, v, flat_near(v, sizes[level][2]))
+        per_probe(fn)
         finish(level, par, field)
         return par
 
@@ -302,9 +323,7 @@
         par = steps[0] % 2
 
         def fn(p):
-            v = w0[...] * rhs[p]
-            v0[p] = v
-            pack(0, par, v, p)
+            pack(0, par, v0, w0[...] * rhs[p], p)
         return fn
 
     XG, ZG = nx * Xc, nz * Zc
@@ -320,70 +339,78 @@
         dd = kk + 6.0 * coup[2]
         d2[...] = dd
         w2[...] = jnp.where(ok, DAMP / dd, 0.0)
-        c3 = pool(kk).reshape(XG // 2, ZG // 2, LANES)
-        lane = iota(c3.shape, 2)
+        kc = pool(kk).reshape(XG // 2, ZG // 2, LANES)
+        lane = iota(kc.shape, 2)
         gy0 = lane + (me["gy"] - reach) * (Yc // 2)
         ok = (lane < WY // 2) & (gy0 >= 0) & (gy0 < ny * (Yc // 2))
-        k3[...] = jnp.where(ok, DAMP / (c3 + 6.0 * coup[3]), 0.0)
+        k3[...] = jnp.where(ok, DAMP / (kc + 6.0 * coup[3]), 0.0)
 
     def coarse_part(which):
         src = gr.at[which]
         unpack(src, b2, probes)
 
-        def fn(p):
+        def down2(p):
             b = b2[p]
             w = w2[...]
             v = w * b
             v = (1.0 - DAMP) * v + w * (b + coup[2] * flat_near(v, WY))
+            v2[p] = v
             r = b - d2[...] * v + coup[2] * flat_near(v, WY)
             r = jnp.where(w > 0.0, r, 0.0)
-            c = pool(r).reshape(XG // 2, ZG // 2, LANES)
-            w3 = k3[...]
-            u = w3 * c
-            for _ in range(COARSE_SWEEPS - 1):
-                u = (1.0 - DAMP) * u + w3 * (c + coup[3] * flat_near(u, WY // 2))
-            e = spread(u.reshape(XG // 2 * (ZG // 2), LANES), XG // 2, ZG // 2, spread_m)
-            v = v + jnp.where(w > 0.0, e, 0.0)
+            c3[p] = pool(r).reshape(XG // 2, ZG // 2, LANES)
+        per_probe(down2)
+        w3 = k3[...]
+        us = [w3 * c3[p] for p in range(probes)]
+        for _ in range(COARSE_SWEEPS - 1):
+            us = [(1.0 - DAMP) * u + w3 * (c3[p] + coup[3] * flat_near(u, WY // 2))
+                  for p, u in enumerate(us)]
+        for p in range(probes):
+            c3[p] = us[p]
+
+        def up2(p):
+            b = b2[p]
+            w = w2[...]
+            e = spread(c3[p].reshape(XG // 2 * (ZG // 2), LANES), XG // 2, ZG // 2, spread_m)
+            v = v2[p] + jnp.where(w > 0.0, e, 0.0)
             for _ in range(2):
                 v = (1.0 - DAMP) * v + w * (b + coup[2] * flat_near(v, WY))
             v2[p] = v
-        per_probe(fn)
+        per_probe(up2)
 
     def sweep(level, rhs, field, more=True):
-        par = exchange(level, field)
         d, w = (d0, d1)[level], (w0, w1)[level]
+
+        def inner(p, v, n):
+            return (1.0 - DAMP) * v + w[...] * (rhs[p] + coup[level] * n)
+        par = exchange(level, field, inner)
         nxt = steps[level] % 2
 
         def fn(p):
-            v = field[p]
-            v = (1.0 - DAMP) * v + w[...] * (rhs[p] + coup[level] * near(level, par, v, p))
-            field[p] = v
+            v = acc[level][p] + w[...] * (coup[level] * halo(level, par, p))
             if more:
-                pack(level, nxt, v, p)
+                pack(level, nxt, field, v, p)
+            else:
+                field[p] = v
         per_probe(fn)
 
     def vcycle(rhs, which):
         per_probe(first(rhs))
         sweep(0, rhs, v0)
-        par = exchange(0, v0)
+        par = exchange(0, v0, lambda p, v, n: rhs[p] - d0[...] * v + n)
         par1 = steps[1] % 2
 
         def down(p, par=par):
-            v = v0[p]
-            r = rhs[p] - d0[...] * v + near(0, par, v, p)
+            r = acc[0][p] + halo(0, par, p)
             b = pool(r).reshape(X1, Z1, LANES)
             b1[p] = b
-            v = w1[...] * b
-            v1[p] = v
-            pack(1, par1, v, p)
+            pack(1, par1, v1, w1[...] * b, p)
         per_probe(down)
         sweep(1, b1, v1)
-        par = exchange(1, v1)
+        par = exchange(1, v1, lambda p, v, n: b1[p] - d1[...] * v + coup[1] * n)
         gsend[which] = jnp.zeros((rows2, LANES), F32)
 
         def down1(p, par=par):
-            v = v1[p]
-            r = b1[p] - d1[...] * v + coup[1] * near(1, par, v, p)
+            r = acc[1][p] + coup[1] * halo(1, par, p)
             r = jnp.where(lv1, r, 0.0)
             gsend[which] = gsend[which] + pltpu.roll(pool(r), p * Yc, 1)
         per_probe(down1)
@@ -398,8 +425,7 @@
             for x in range(Xc):
                 e3[pl.ds(x * Zc, Zc), :] = v2[p, me["gx"] * Xc + x, pl.ds(me["gz"] * Zc, Zc), :]
             v = v1[p] + spread(e3[...], Xc, Zc, own_m)
-            v1[p] = v
-            pack(1, nxt, v, p)
+            pack(1, nxt, v1, v, p)
         per_probe(up1)
         sweep(1, b1, v1)
         sweep(1, b1, v1, more=False)
@@ -407,21 +433,20 @@
 
         def up0(p):
             v = v0[p] + spread(v1[p].reshape(X1 * Z1, LANES), X1, Z1, spread_m)
-            v0[p] = v
-            pack(0, nxt0, v, p)
+            pack(0, nxt0, v0, v, p)
         per_probe(up0)
         sweep(0, rhs, v0)
-        sweep(0, rhs, v0)
+        sweep(0, rhs, v0, more=which == 0)
 
     def begin(p):
         r0[p] = 2.0 * bits[p].astype(F32) - 1.0
     per_probe(begin)
     vcycle(r0, 0)
-    par = exchange(0, v0)
+    par = exchange(0, v0, lambda p, v, n: d0[...] * v - n)
 
     def image(p, row, par=par):
         v = v0[p]
-        q = d0[...] * v - near(0, par, v, p)
+        q = acc[0][p] - halo(0, par, p)
         p0[p] = v
         q0[p] = q
         row = put(row, 0, p, r0[p] * v)
@@ -435,15 +460,14 @@
     def direction(p):
         a = get(sums0, 0, p) / get(sums0, 1, p)
         v = p0[p] - a * v0[p]
-        v0[p] = v
         r0[p] = r0[p] - a * q0[p]
-        pack(0, nxt, v, p)
+        pack(0, nxt, v0, v, p)
     per_probe(direction)
-    par = exchange(0, v0)
+    par = exchange(0, v0, lambda p, v, n: d0[...] * v - n)
 
     def image2(p, row, par=par):
         v = v0[p]
-        t = d0[...] * v - near(0, par, v, p)
+        t = acc[0][p] - halo(0, par, p)
         b0[p] = t
         row = put(row, 0, p, r0[p] * v)
         row = put(row, 1, p, v * t)
@@ -493,7 +517,7 @@
     def halo(level):
         x, z, _ = sizes[level]
         return [vm(2, 2, probes, z, LANES), vm(2, 2, probes, x, 1, LANES),
-                vm(2, 2, probes, x, 1, LANES), vm(2, 2, z, LANES), vm(2, 2, z, LANES)]
+                vm(2, 2, probes, x, 1, LANES), vm(2, z, LANES), vm(2, 2, z, LANES), vm(z, LANES)]
 
     dma = pltpu.SemaphoreType.DMA
     scratch = [full(0), full(0), full(0), full(0), full(0), coef(0), coef(0),
@@ -505,6 +529,7 @@
                vm(probes, XG, ZG, LANES), vm(probes, XG, ZG, LANES), vm(1, XG, ZG, LANES),
                vm(XG, ZG, LANES), vm(probes, XG // 2, ZG // 2, LANES), vm(XG, ZG, LANES),
                vm(XG // 2, ZG // 2, LANES), vm(Xc * Zc, LANES),
+               vm(probes, XG // 2, ZG // 2, LANES), full(1),
                vm(3, 1, LANES), vm(3, total, 1, LANES), dma((3, total)), dma((3, total))]
     cfg = (probes, sizes, mesh_counts, reach, width)
     field, rel = pl.pallas_call(

time: 134 us -> 114 us (0.85)
  Pallas kernels: 130 us -> 110 us
    pallas_call x1, Pallas kernels: 130 us -> 110 us  [per_device(): pl.pallas_call(functools.partial(body, cfg), out_shape=(jax.ShapeDtypeStr...]
where the time goes in v2:
time: 114 us
  Pallas kernels  110 us (96%)
  local copies, waits for them, and re-layouts  3.24 us (3%)
    pallas_call x1, Pallas kernels, per_device(): pl.pallas_call(functools.partial(body, cfg), out_shape=(jax.ShapeDtypeStr...  110 us
    unnamed x5, local copies, waits for them, and re-layouts  2.73 us

profile of v2, /device:TPU:0, one launch (start us, length us, event | category | flops | bytes accessed | tf_op | source)
XLA Modules:
  0.0 114.0 jit_solution(16250536340502390202)
XLA Ops:
  0.6 0.0 copy-start
  0.6 1.0 copy-done
  1.7 0.0 copy-start.1
  1.7 0.9 copy-done.1
  2.6 110.1 %shard_map.41 = (f32[4,16,16,128]{3,2,1,0:T(8,128)S(1)}, f32[1,128]{1,0:T(1,128)S(1)}) custom-call(f32[16,16,128]{2,1,0:T(8,128)S(1)} %copy-done.1, s32[4,16,16,128]{3,2,1,0:T(8,128)S(1)} %copy-done), custom_call_target="tpu_custom_call" | custom-call | tf_op jit(solution)/shard_map/pallas_call | solution.py:535
  112.7 0.5 slice_bitcast_fusion
  113.2 0.8 copy.5
Async XLA Ops:
  0.6 1.0 copy-start
  1.7 0.9 copy-start.1

commit v3 on v2

--- a/solution.py
+++ b/solution.py
@@ -46,21 +46,23 @@
     y2 = sizes[2][2]
     own_m = jnp.where((ci // 2 + reach * y2 == ri) & (ci < 2 * y2), 1.0, 0.0).astype(F32)
 
-    def pool(f):
+    def pool(f, k=0):
         cx, cz, _ = f.shape
         s = f.reshape(cx // 2, 2, cz, LANES)
         s = (s[:, 0] + s[:, 1]).reshape(cx // 2 * cz, LANES)
         rows = cx // 2 * cz
-        tmp[pl.ds(0, rows), :] = s
-        h = tmp[pl.ds(0, rows // 2, stride=2), :] + tmp[pl.ds(1, rows // 2, stride=2), :]
+        t = tmp.at[k]
+        t[pl.ds(0, rows), :] = s
+        h = t[pl.ds(0, rows // 2, stride=2), :] + t[pl.ds(1, rows // 2, stride=2), :]
         return dot(h, pool_m)
 
-    def spread(e, cx, cz, mat):
+    def spread(e, cx, cz, mat, k=0):
         rows = cx * cz
         f = dot(e, mat)
-        tmp[pl.ds(0, rows, stride=2), :] = f
-        tmp[pl.ds(1, rows, stride=2), :] = f
-        g = tmp[pl.ds(0, 2 * rows), :].reshape(cx, 1, 2 * cz, LANES)
+        t = tmp.at[k]
+        t[pl.ds(0, rows, stride=2), :] = f
+        t[pl.ds(1, rows, stride=2), :] = f
+        g = t[pl.ds(0, 2 * rows), :].reshape(cx, 1, 2 * cz, LANES)
         return jnp.broadcast_to(g, (cx, 2, 2 * cz, LANES)).reshape(2 * cx, 2 * cz, LANES)
 
     def face_copies(level, par, field, axes, p=None):
@@ -114,19 +116,20 @@
         X, _, Y = sizes[level]
         return 2 * (p * X + x) + 1 if Y == LANES else p * X + x
 
-    def pack(level, par, field, v, p):
+    def pack(level, par, field, v, p, send=True):
         X, Z, Y = sizes[level]
         field[p] = v
         zs[level][par, 0, p] = v[:, 0:1, :]
         zs[level][par, 1, p] = v[:, Z - 1 : Z, :]
-        start(level, par, field, (0, 1), p)
         lane = iota((Z, LANES), 1)
         tile = ys[level][par]
         for x in range(X):
             s = lane_of(level, p, x)
-            hit = (lane == s) | (lane == lax.rem(s + Y - 1, LANES))
+            hit = (lane == s) | (lane == (s + Y - 1) % LANES)
             tile = jnp.where(hit, pltpu.roll(v[x], s, 1), tile)
         ys[level][par] = tile
+        if send:
+            start(level, par, field, (0, 1), p)
 
     def halo(level, par, p):
         X, Z, Y = sizes[level]
@@ -135,7 +138,7 @@
         m = ym[level][...]
         planes = []
         for x in range(X):
-            back = lax.rem(2 * LANES - lane_of(level, p, x), LANES)
+            back = (2 * LANES - lane_of(level, p, x)) % LANES
             h = jnp.where(edge, pltpu.roll(m, back, 1), 0.0)
             h = h + jnp.where(sub == 0, zr[level][par, 0, p, x],
                               jnp.where(sub == Z - 1, zr[level][par, 1, p, x], 0.0))
@@ -157,7 +160,12 @@
         n = n + jnp.where(lane >= Y - 1, 0.0, pltpu.roll(v, LANES - 1, 2))
         return n
 
-    def per_probe(fn):
+    def per_probe(fn, unroll=False):
+        if unroll:
+            for p in range(probes):
+                fn(p)
+            return
+
         def step(p, c):
             fn(p)
             return c
@@ -173,7 +181,7 @@
         def fn(p):
             v = field[p]
             acc[level][p] = inner(p, v, flat_near(v, sizes[level][2]))
-        per_probe(fn)
+        per_probe(fn, level == 1)
         finish(level, par, field)
         return par
 
@@ -388,10 +396,12 @@
         def fn(p):
             v = acc[level][p] + w[...] * (coup[level] * halo(level, par, p))
             if more:
-                pack(level, nxt, field, v, p)
+                pack(level, nxt, field, v, p, level == 0)
             else:
                 field[p] = v
-        per_probe(fn)
+        per_probe(fn, level == 1)
+        if more and level == 1:
+            start(level, nxt, field, (0, 1))
 
     def vcycle(rhs, which):
         per_probe(first(rhs))
@@ -407,13 +417,14 @@
         per_probe(down)
         sweep(1, b1, v1)
         par = exchange(1, v1, lambda p, v, n: b1[p] - d1[...] * v + coup[1] * n)
-        gsend[which] = jnp.zeros((rows2, LANES), F32)
+        rows = []
 
         def down1(p, par=par):
             r = acc[1][p] + coup[1] * halo(1, par, p)
             r = jnp.where(lv1, r, 0.0)
-            gsend[which] = gsend[which] + pltpu.roll(pool(r), p * Yc, 1)
-        per_probe(down1)
+            rows.append(pltpu.roll(pool(r, p), p * Yc, 1))
+        per_probe(down1, True)
+        gsend[which] = functools.reduce(jnp.add, rows)
         gather_start(gr.at[which], grs.at[which], which)
         if which == 0:
             coefs2()
@@ -423,10 +434,11 @@
 
         def up1(p):
             for x in range(Xc):
-                e3[pl.ds(x * Zc, Zc), :] = v2[p, me["gx"] * Xc + x, pl.ds(me["gz"] * Zc, Zc), :]
-            v = v1[p] + spread(e3[...], Xc, Zc, own_m)
-            pack(1, nxt, v1, v, p)
-        per_probe(up1)
+                e3[p, pl.ds(x * Zc, Zc), :] = v2[p, me["gx"] * Xc + x, pl.ds(me["gz"] * Zc, Zc), :]
+            v = v1[p] + spread(e3[p], Xc, Zc, own_m, p)
+            pack(1, nxt, v1, v, p, False)
+        per_probe(up1, True)
+        start(1, nxt, v1, (0, 1))
         sweep(1, b1, v1)
         sweep(1, b1, v1, more=False)
         nxt0 = steps[0] % 2
@@ -469,9 +481,12 @@
         v = v0[p]
         t = acc[0][p] - halo(0, par, p)
         b0[p] = t
-        row = put(row, 0, p, r0[p] * v)
-        row = put(row, 1, p, v * t)
-        return put(row, 2, p, v * q0[p])
+        r, q = r0[p], q0[p]
+        a = get(sums0, 0, p) / get(sums0, 1, p)
+        g = r - a * t
+        for k, f in enumerate((r * v, v * t, v * q, g * g, g * t, g * q, t * t, t * q, q * q)):
+            row = put(row, k, p, f)
+        return row
     row = lax.fori_loop(0, probes, image2, jnp.zeros((1, LANES), F32))
     reduce_start(1, row)
     sums1 = reduce_finish(1)
@@ -479,16 +494,17 @@
     def final(p, row):
         rz0, pq0 = get(sums0, 0, p), get(sums0, 1, p)
         rz1, pt, pq = get(sums1, 0, p), get(sums1, 1, p), get(sums1, 2, p)
+        gg, gt, gq, tt, tq, qq = [get(sums1, k, p) for k in range(3, 9)]
         a0 = rz0 / pq0
         beta = rz1 / rz0
         a1 = rz1 / (pt + 2.0 * beta * pq + beta * beta * pq0)
         x_out[p] = a0 * p0[p] + a1 * (v0[p] + beta * p0[p])
-        r = r0[p] - a1 * (b0[p] + beta * q0[p])
-        return put(row, 0, p, r * r)
+        c, h = a1 - a0, a1 * beta
+        sq = gg - 2.0 * c * gt - 2.0 * h * gq + c * c * tt + 2.0 * c * h * tq + h * h * qq
+        return jnp.where(lane1 == p, sq, row)
     row = lax.fori_loop(0, probes, final, jnp.zeros((1, LANES), F32))
-    reduce_start(2, row)
     cells = float(X0 * Z0 * Y0 * total)
-    rel_out[...] = jnp.sqrt(reduce_finish(2) / cells)
+    rel_out[...] = jnp.sqrt(jnp.maximum(row, 0.0) / cells)
 
 
 def per_device(mesh_counts, kappa_sq, probe_bits):
@@ -498,7 +514,7 @@
     reach = min(math.ceil(need / sizes[2][2]), mesh_counts["gy"] - 1)
     width = 2 * reach + 1
     assert Y <= LANES and width * sizes[2][2] <= LANES and probes * X <= LANES
-    assert probes * sizes[2][2] <= LANES
+    assert probes * sizes[2][2] <= LANES and 9 * probes <= LANES
     nx, nz, ny = mesh_counts["gx"], mesh_counts["gz"], mesh_counts["gy"]
     total = nx * nz * ny
     slots = nx * nz * width
@@ -523,14 +539,14 @@
     scratch = [full(0), full(0), full(0), full(0), full(0), coef(0), coef(0),
                full(1), full(1), coef(1), coef(1), *halo(0), *halo(1),
                dma((2, 2, 3, 2)), dma((2, 2, 3, 2)),
-               vm(max(X * Z, XG * ZG), LANES), vm(3, Xc * Zc, LANES),
+               vm(probes, max(X * Z, XG * ZG), LANES), vm(3, Xc * Zc, LANES),
                vm(slots, Xc * Zc, LANES), vm(2, slots, Xc * Zc, LANES),
                dma((3, slots)), dma((slots,)), dma((2, slots)),
                vm(probes, XG, ZG, LANES), vm(probes, XG, ZG, LANES), vm(1, XG, ZG, LANES),
                vm(XG, ZG, LANES), vm(probes, XG // 2, ZG // 2, LANES), vm(XG, ZG, LANES),
-               vm(XG // 2, ZG // 2, LANES), vm(Xc * Zc, LANES),
+               vm(XG // 2, ZG // 2, LANES), vm(probes, Xc * Zc, LANES),
                vm(probes, XG // 2, ZG // 2, LANES), full(1),
-               vm(3, 1, LANES), vm(3, total, 1, LANES), dma((3, total)), dma((3, total))]
+               vm(2, 1, LANES), vm(2, total, 1, LANES), dma((2, total)), dma((2, total))]
     cfg = (probes, sizes, mesh_counts, reach, width)
     field, rel = pl.pallas_call(
         functools.partial(body, cfg),

time: 114 us -> 106 us (0.930)
  Pallas kernels: 110 us -> 102 us
    pallas_call x1, Pallas kernels: 110 us -> 102 us  [per_device(): pl.pallas_call(functools.partial(body, cfg), out_shape=(jax.ShapeDtypeStr...]
where the time goes in v3:
time: 106 us
  Pallas kernels  102 us (96%)
  local copies, waits for them, and re-layouts  3.24 us (3%)
    pallas_call x1, Pallas kernels, per_device(): pl.pallas_call(functools.partial(body, cfg), out_shape=(jax.ShapeDtypeStr...  102 us
    unnamed x5, local copies, waits for them, and re-layouts  2.73 us

profile of v3, /device:TPU:0, one launch (start us, length us, event | category | flops | bytes accessed | tf_op | source)
XLA Modules:
  0.0 106.0 jit_solution(602553388901585211)
XLA Ops:
  0.6 0.0 copy-start
  0.6 1.0 copy-done
  1.7 0.0 copy-start.1
  1.7 0.9 copy-done.1
  2.6 102.1 %shard_map.41 = (f32[4,16,16,128]{3,2,1,0:T(8,128)S(1)}, f32[1,128]{1,0:T(1,128)S(1)}) custom-call(f32[16,16,128]{2,1,0:T(8,128)S(1)} %copy-done.1, s32[4,16,16,128]{3,2,1,0:T(8,128)S(1)} %copy-done), custom_call_target="tpu_custom_call" | custom-call | tf_op jit(solution)/shard_map/pallas_call | solution.py:551
  104.7 0.5 slice_bitcast_fusion
  105.2 0.8 copy.5
Async XLA Ops:
  0.6 1.0 copy-start
  1.7 0.9 copy-start.1
